TPU v7x, 128 devices: a whole 4x4x4 slice. The times are simulated.
128 devices in a mesh: row: 8 (over z, core), col: 16 (over y, x).
Axes of the slice: x: 4, y: 4, z: 4, core: 2. Of those that a mesh axis runs over, the one named last changes fastest.
Arguments:
- clean: float32 [1344, 16384], P('row', 'col'), may hold values from -6 to 6
- noise: float32 [1344, 16384], P('row', 'col'), may hold values from -6 to 6
- bucket: int32 [64], replicated, may hold values from 0 to 31
- mod_table: float32 [1, 32, 1344], replicated, may hold values from -3 to 3
- w_first: float32 [1, 1344, 1344], P(None, 'row', 'col'), may hold values from -0.15625 to 0.15625
- w_second: float32 [1, 1344, 1344], P(None, 'col', 'row'), may hold values from -0.15625 to 0.15625
Outputs:
- grad_first: float32 [1, 1344, 1344], P(None, 'row', 'col')
- grad_second: float32 [1, 1344, 1344], P(None, 'col', 'row')
All inputs are finite; a program needn't handle non-finite values.
Results may differ from a plain program's by a relative error of at most 0.018.
Values may be sent and summed in bfloat16 or wider, within the bound.
A program may use at most 64 MiB of HBM per device.

v0:
```python
import math
import jax
import jax.numpy as jnp
from jax import lax
from jax.sharding import Mesh
from jax.sharding import PartitionSpec as P

PIX = 256
BUCKETS = 32
COL = ("col_0", "col_1")
MIX_WEIGHT = 0.3
KEEP_COEF = (1.0 - MIX_WEIGHT) / math.sqrt((1.0 - MIX_WEIGHT) ** 2 + MIX_WEIGHT**2)
ADD_COEF = MIX_WEIGHT / math.sqrt((1.0 - MIX_WEIGHT) ** 2 + MIX_WEIGHT**2)
SILU_GAIN = 1.0 / 0.596
CONTRACT_LEAD = (((0,), (0,)), ((), ()))
CONTRACT_TAIL = (((1,), (1,)), ((), ()))


def sent_to_all(value, axis):
    copies = jnp.broadcast_to(value, (lax.axis_size(axis), *value.shape))
    return lax.all_to_all(copies, axis, split_axis=0, concat_axis=0, tiled=True)


def over_copies(value, axis):
    everything = sent_to_all(value, axis)
    return jnp.sum(everything, axis=0)


def one_axis_at_a_time(value, axes):
    for axis in axes:
        value = lax.psum(value, axis)
    return value


def rows_first(arrays, axis, dims):
    turned = [jnp.moveaxis(a, dim, 0) for a, dim in zip(arrays, dims)]
    widths = [t[0].size for t in turned]
    both = jnp.concatenate([t.reshape(-1, w) for t, w in zip(turned, widths)], axis=1)
    result = lax.all_gather(both, axis, axis=0, tiled=True)
    blocks = jnp.split(result, [sum(widths[:k]) for k in range(1, len(widths))], axis=1)
    return tuple(
        (
            jnp.moveaxis(b.reshape(-1, *t.shape[1:]), 0, dim)
            for b, t, dim in zip(blocks, turned, dims)
        )
    )


def split_up(value, dim, count):
    before, after = (value.shape[:dim], value.shape[dim + 1 :])
    return jnp.moveaxis(value.reshape(*before, count, -1, *after), dim, 0)


def sum_together(arrays, axis, dims):
    count = lax.axis_size(axis)
    blocks = [split_up(a, dim, count) for a, dim in zip(arrays, dims)]
    lines = jnp.concatenate([b.reshape(count, -1) for b in blocks], axis=1)
    extent = max(16, -(-lines.shape[1] // 1024) * 8)
    lines = jnp.pad(lines, ((0, 0), (0, extent * 128 - lines.shape[1]))).reshape(-1, 128)
    ravelled, at, gathered = (lax.psum_scatter(lines, axis, tiled=True).reshape(-1), 0, [])
    for b in blocks:
        part = b[0]
        gathered.append(ravelled[at : at + part.size].reshape(part.shape))
        at += part.size
    return tuple(gathered)


def noise_levels(bucket):
    return jnp.exp(-3.0 + 5.0 * (bucket.astype(jnp.float32) + 0.5) / BUCKETS)


def silu_slope(values):
    sig = jax.nn.sigmoid(values)
    return sig * (1.0 + values * (1.0 - sig))


def bucket_gains(table, picked):
    onehot = (picked[:, None] == jnp.arange(table.shape[0], dtype=jnp.int32)[None, :]).astype(
        jnp.float32
    )
    return jnp.dot(onehot, table, preferred_element_type=jnp.float32)


def local(clean, noise, bucket, mod_table, w_first, w_second):
    rows_size = lax.axis_size("row")
    row_at = lax.axis_index("row")
    col_at = lax.axis_index(COL)
    samples = bucket.shape[0]
    own_rows = clean.shape[1]
    weight_first = w_first[0]
    weight_second = w_second[0]
    table = 1.0 + mod_table[0]
    col_first = jnp.sqrt(over_copies(jnp.sum(weight_first * weight_first, axis=0), "row") + 1.0)
    col_second = jnp.sqrt(
        one_axis_at_a_time(jnp.sum(weight_second * weight_second, axis=0), COL) + 1.0
    )
    normed_first = (weight_first / col_first[None, :]).astype(jnp.bfloat16)
    normed_second = (weight_second / col_second[None, :]).astype(jnp.bfloat16)
    chan_clean, chan_noise = (
        lax.all_to_all(
            clean.astype(jnp.bfloat16), "row", split_axis=1, concat_axis=0, tiled=True
        ).astype(clean.dtype),
        lax.all_to_all(
            noise.astype(jnp.bfloat16), "row", split_axis=1, concat_axis=0, tiled=True
        ).astype(noise.dtype),
    )
    local_clean = chan_clean.T
    local_noise = chan_noise.T
    sub_rows = own_rows // rows_size
    first_row = col_at * own_rows + row_at * sub_rows
    row_sample = (first_row + jnp.arange(sub_rows, dtype=jnp.int32)) // PIX
    row_bucket = jnp.take(bucket, row_sample)
    levels = noise_levels(row_bucket)[:, None]
    spread_root = jnp.sqrt(levels * levels + 0.25)
    state_own = ((local_clean + levels * local_noise) / spread_root).astype(jnp.bfloat16)
    target = local_clean * (2.0 * levels / spread_root) - local_noise * (0.5 / spread_root)
    gains = bucket_gains(table, row_bucket)
    part_first, part_second = rows_first((normed_first, normed_second), COL, (1, 0))
    full_first, full_second = rows_first((part_first, part_second), "row", (0, 1))
    pre_act = jnp.dot(state_own, full_first, preferred_element_type=jnp.float32)
    hidden = (jax.nn.silu(pre_act) * SILU_GAIN * gains).astype(jnp.bfloat16)
    branch = jnp.dot(hidden, full_second, preferred_element_type=jnp.float32)
    state_new = (KEEP_COEF * state_own.astype(jnp.float32) + ADD_COEF * branch).astype(jnp.bfloat16)
    grad_own = (state_new.astype(jnp.float32) - target) / samples
    dbranch = (ADD_COEF * grad_own).astype(jnp.bfloat16)
    gsecond_full = lax.dot_general(
        hidden, dbranch, CONTRACT_LEAD, preferred_element_type=jnp.float32
    )
    dhidden = lax.dot_general(
        dbranch, full_second, CONTRACT_TAIL, preferred_element_type=jnp.float32
    )
    dpre = (dhidden * gains * silu_slope(pre_act) * SILU_GAIN).astype(jnp.bfloat16)
    gfirst_full = lax.dot_general(
        state_own, dpre, CONTRACT_LEAD, preferred_element_type=jnp.float32
    )
    part_gfirst, part_gsecond = (
        lax.psum_scatter(
            gfirst_full.astype(jnp.bfloat16), COL, scatter_dimension=1, tiled=True
        ).astype(jnp.float32),
        lax.psum_scatter(
            gsecond_full.astype(jnp.bfloat16), COL, scatter_dimension=0, tiled=True
        ).astype(jnp.float32),
    )
    gfirst, gsecond = tuple(
        (
            part.astype(jnp.float32)
            for part in sum_together(
                (part_gfirst.astype(jnp.bfloat16), part_gsecond.astype(jnp.bfloat16)), "row", (0, 1)
            )
        )
    )
    dot_first = over_copies(jnp.sum(weight_first * gfirst, axis=0), "row")
    dot_second = one_axis_at_a_time(jnp.sum(weight_second * gsecond, axis=0), COL)
    grad_first = gfirst / col_first[None, :] - weight_first * (dot_first / col_first**3)[None, :]
    grad_second = (
        gsecond / col_second[None, :] - weight_second * (dot_second / col_second**3)[None, :]
    )
    return (grad_first[None], grad_second[None])


def solution(mesh):
    torus = Mesh(mesh.devices.reshape(mesh.shape["row"], 4, 4), ("row", "col_0", "col_1"))
    in_specs = (P("row", COL), P("row", COL), P(), P(), P(None, "row", COL), P(None, COL, "row"))
    out_specs = (P(None, "row", COL), P(None, COL, "row"))
    return jax.shard_map(local, mesh=torus, in_specs=in_specs, out_specs=out_specs, check_vma=False)
```

profile of v0, /device:TPU:1, one launch (start us, length us, event | category | flops | bytes accessed | tf_op | source)
XLA Modules:
  0.0 332.8 jit_solution(9308178163140917538)
XLA Ops:
  8.7 6.8 %all-to-all-start.2 = ((f32[8,1,84]{2,1,0:T(1,128)}), f32[8,1,84]{2,1,0:T(1,128)S(1)}, u32[]{:S(2)}, u32[]{:S(2)}) async-start(f32[8,1,84]{2,1,0:T(1,128)} %broadcast_in_dim.11), calls=%async_computation.2 | async-start | bytes 8192 | tf_op jit(solution)/shard_map/all_to_all | solution.py:21
  16.6 8.7 %psum.28 = f32[168]{0:T(256)S(1)} all-reduce(f32[168]{0:T(256)S(1)} %fusion.60), channel_id=1, replica_groups=mesh['row'=8,'col_0'=4,'col_1'=4] {'col_0'}, use_global_device_ids=true, to_apply=%region_3.0 | all-reduce | flops 168 | bytes 1344 | tf_op jit(solution)/shard_map/psum | solution.py:31
  25.3 8.5 %psum.29 = f32[168]{0:T(256)S(1)} all-reduce(f32[168]{0:T(256)S(1)} %psum.28), channel_id=1, replica_groups=mesh['row'=8,'col_0'=4,'col_1'=4] {'col_1'}, use_global_device_ids=true, to_apply=%region_4.0 | all-reduce | flops 168 | bytes 1344 | tf_op jit(solution)/shard_map/psum | solution.py:31
  35.0 17.3 %all-gather = bf16[16,84,336]{2,1,0:T(8,128)(2,1)S(1)} all-gather(bf16[1,84,336]{2,1,0:T(8,128)(2,1)S(1)} %copy.38), channel_id=1, replica_groups=mesh['row'=8,'col_0'=4,'col_1'=4] {'col_0','col_1'}, dimensions={0}, use_global_device_ids=true | all-gather | bytes 959616 | tf_op jit(solution)/shard_map/all_gather | solution.py:39
  55.9 13.5 %all-to-all-start = ((bf16[168,8,128]{2,0,1:T(8,128)(2,1)}), bf16[168,8,128]{2,0,1:T(8,128)(2,1)S(1)}, u32[]{:S(2)}, u32[]{:S(2)}) async-start(bf16[168,8,128]{2,0,1:T(8,128)(2,1)} %copy_bitcast_fusion.2), calls=%async_computation | async-start | bytes 688128 | tf_op jit(solution)/shard_map/all_to_all | solution.py:100
  71.5 5.1 %all-to-all-done = bf16[168,8,128]{2,0,1:T(8,128)(2,1)S(1)} async-done(((bf16[168,8,128]{2,0,1:T(8,128)(2,1)}), bf16[168,8,128]{2,0,1:T(8,128)(2,1)S(1)}, u32[]{:S(2)}, u32[]{:S(2)}) %all-to-all-start) | async-done | bytes 344096 | tf_op jit(solution)/shard_map/all_to_all | solution.py:100
  76.6 4.5 %all-to-all-start.1 = ((bf16[168,8,128]{2,0,1:T(8,128)(2,1)}), bf16[168,8,128]{2,0,1:T(8,128)(2,1)S(1)}, u32[]{:S(2)}, u32[]{:S(2)}) async-start(bf16[168,8,128]{2,0,1:T(8,128)(2,1)} %copy_bitcast_fusion.1), calls=%async_computation.1 | async-start | bytes 688128 | tf_op jit(solution)/shard_map/all_to_all | solution.py:103
  81.2 11.6 %all-to-all-done.1 = bf16[168,8,128]{2,0,1:T(8,128)(2,1)S(1)} async-done(((bf16[168,8,128]{2,0,1:T(8,128)(2,1)}), bf16[168,8,128]{2,0,1:T(8,128)(2,1)S(1)}, u32[]{:S(2)}, u32[]{:S(2)}) %all-to-all-start.1) | async-done | bytes 344096 | tf_op jit(solution)/shard_map/all_to_all | solution.py:103
  93.0 19.6 %all-gather.3.cloned.1.call-done = bf16[1344,2688]{1,0:T(8,128)(2,1)} async-done(((bf16[168,2688]{1,0:T(8,128)(2,1)}), bf16[1344,2688]{1,0:T(8,128)(2,1)}) %all-gather.3.cloned.1.call-update) | async-done | bytes 7225360 | tf_op jit(solution)/shard_map/all_gather | solution.py:39
  112.7 3.9 %fusion.2 = f32[128,1344]{0,1:T(8,128)S(1)} fusion(bf16[1344,128]{1,0:T(8,128)(2,1)S(1)} %get-tuple-element.12, bf16[1344,2688]{1,0:T(8,128)(2,1)} %all-gather.3.cloned.1.call-done), kind=kOutput, calls=%fused_computation.3 | convolution fusion | flops 462422016 | bytes 4816896 | tf_op jit(solution)/shard_map/dot_general | solution.py:120
  119.4 3.1 convolution_convert_fusion
  122.5 8.7 %convolution_convert_fusion.1 = bf16[1344,1344]{0,1:T(8,128)(2,1)} fusion(bf16[1344,128]{1,0:T(8,128)(2,1)S(1)} %get-tuple-element.12, f32[128,1344]{0,1:T(8,128)S(1)} %copy-done.8, bf16[128,1344]{0,1:T(8,128)(2,1)S(1)} %fusion.38, bf16[1344,2688]{1,0:T(8,128)(2,1)} %all-gather.3.cloned.1.call-done, f32[128,1344]{0,1:T(8,128)S(1)} %fusion.2), kind=kOutput, calls=%fused_computation.2 | convolution fusion | flops 928542720 | bytes 9461760 | tf_op jit(solution)/shard_map/dot_general | solution.py:133
  131.2 101.1 %fusion.75 = (bf16[96,1344]{1,0:T(8,128)(2,1)S(1)}, bf16[1344,96]{0,1:T(8,128)(2,1)S(1)}) fusion(bf16[1344,1344]{1,0:T(8,128)(2,1)} %convolution_convert_fusion, bf16[1344,1344]{0,1:T(8,128)(2,1)} %convolution_convert_fusion.1), kind=kCustom, calls=%all-reduce-scatter.2 | all-reduce-scatter fusion | flops 4128769 | bytes 7741952
  232.3 2.8 collective-permute-start
  236.5 4.2 %collective-permute-start.2 = (bf16[96,1344]{1,0:T(8,128)(2,1)S(1)}, bf16[96,1344]{1,0:T(8,128)(2,1)S(1)}, u32[]{:S(2)}, u32[]{:S(2)}) collective-permute-start(bf16[96,1344]{1,0:T(8,128)(2,1)S(1)} %get-tuple-element.4), channel_id=1, source_target_pairs={{0,1},{1,2},{2,3},{3,4},{4,5},{5,6},{6,7},{7,8},{8,9},{9,10},{10,1... | collective-permute-start | bytes 774152
  242.1 2.7 collective-permute-start.3
  245.2 3.1 concatenate.12
  248.9 7.4 %collective-permute-done.3 = bf16[84,1344]{1,0:T(8,128)(2,1)S(1)} collective-permute-done((bf16[84,1344]{1,0:T(8,128)(2,1)S(1)}, bf16[84,1344]{1,0:T(8,128)(2,1)S(1)}, u32[]{:S(2)}, u32[]{:S(2)}) %collective-permute-start.3) | collective-permute-done | bytes 225824
  256.3 3.1 concatenate.13
  261.6 29.3 %reduce-scatter.6.cloned.1.call-done = bf16[224,128]{1,0:T(8,128)(2,1)} async-done(((bf16[1792,128]{1,0:T(8,128)(2,1)}), bf16[224,128]{1,0:T(8,128)(2,1)}) %reduce-scatter.6.cloned.1.call-update) | async-done | bytes 57360 | tf_op jit(solution)/shard_map/reduce_scatter | solution.py:60
  292.3 8.6 %psum.30 = f32[168]{0:T(256)S(1)} all-reduce(f32[168]{0:T(256)S(1)} %fusion.62), channel_id=1, replica_groups=mesh['row'=8,'col_0'=4,'col_1'=4] {'col_0'}, use_global_device_ids=true, to_apply=%region_11.12 | all-reduce | flops 168 | bytes 1344 | tf_op jit(solution)/shard_map/psum | solution.py:31
  300.9 8.4 %psum.31 = f32[168]{0:T(256)S(1)} all-reduce(f32[168]{0:T(256)S(1)} %psum.30), channel_id=1, replica_groups=mesh['row'=8,'col_0'=4,'col_1'=4] {'col_1'}, use_global_device_ids=true, to_apply=%region_12.13 | all-reduce | flops 168 | bytes 1344 | tf_op jit(solution)/shard_map/psum | solution.py:31
  310.1 10.6 %all-to-all-start.3 = ((f32[8,1,84]{2,1,0:T(1,128)}), f32[8,1,84]{2,1,0:T(1,128)S(1)}, u32[]{:S(2)}, u32[]{:S(2)}) async-start(f32[8,1,84]{2,1,0:T(1,128)} %broadcast_in_dim.12), calls=%async_computation.4 | async-start | bytes 8192 | tf_op jit(solution)/shard_map/all_to_all | solution.py:21
  321.6 3.6 %all-to-all-done.3 = f32[8,1,84]{2,1,0:T(1,128)S(1)} async-done(((f32[8,1,84]{2,1,0:T(1,128)}), f32[8,1,84]{2,1,0:T(1,128)S(1)}, u32[]{:S(2)}, u32[]{:S(2)}) %all-to-all-start.3) | async-done | bytes 2720 | tf_op jit(solution)/shard_map/all_to_all | solution.py:21
  (78 shorter events, 21.5 us)
Async XLA Ops:
  7.2 62.3 %copy-start = (s32[64]{0:T(128)S(1)}, s32[64]{0:T(128)}, u32[]{:S(2)}) copy-start(s32[64]{0:T(128)} %param.8) | copy-start | bytes 772
  8.7 25.2 %all-to-all-start.2 = ((f32[8,1,84]{2,1,0:T(1,128)}), f32[8,1,84]{2,1,0:T(1,128)S(1)}, u32[]{:S(2)}, u32[]{:S(2)}) async-start(f32[8,1,84]{2,1,0:T(1,128)} %broadcast_in_dim.11), calls=%async_computation.2 | async-start | bytes 8192 | tf_op jit(solution)/shard_map/all_to_all | solution.py:21
  15.5 97.1 %all-gather.3.cloned.1.call-start = ((), (), s32[]{:S(2)}) async-start(), calls=%async_computation.5 | async-start | bytes 8128512 | tf_op jit(solution)/shard_map/all_gather | solution.py:39
  52.7 2.4 copy-start.2
  53.0 17.7 %copy-start.3 = (f32[168,1024]{1,0:T(8,128)S(1)}, f32[168,1024]{1,0:T(8,128)}, u32[]{:S(2)}) copy-start(f32[168,1024]{1,0:T(8,128)} %param.7) | copy-start | bytes 2064388
  55.9 20.7 %all-to-all-start = ((bf16[168,8,128]{2,0,1:T(8,128)(2,1)}), bf16[168,8,128]{2,0,1:T(8,128)(2,1)S(1)}, u32[]{:S(2)}, u32[]{:S(2)}) async-start(bf16[168,8,128]{2,0,1:T(8,128)(2,1)} %copy_bitcast_fusion.2), calls=%async_computation | async-start | bytes 688128 | tf_op jit(solution)/shard_map/all_to_all | solution.py:100
  76.6 16.2 %all-to-all-start.1 = ((bf16[168,8,128]{2,0,1:T(8,128)(2,1)}), bf16[168,8,128]{2,0,1:T(8,128)(2,1)S(1)}, u32[]{:S(2)}, u32[]{:S(2)}) async-start(bf16[168,8,128]{2,0,1:T(8,128)(2,1)} %copy_bitcast_fusion.1), calls=%async_computation.1 | async-start | bytes 688128 | tf_op jit(solution)/shard_map/all_to_all | solution.py:103
  81.1 35.4 %copy-start.7 = (f32[1,32,1344]{2,1,0:T(8,128)S(1)}, f32[1,32,1344]{2,1,0:T(8,128)}, u32[]{:S(2)}) copy-start(f32[1,32,1344]{2,1,0:T(8,128)} %param.9) | copy-start | bytes 516100
  81.1 209.7 %reduce-scatter.6.cloned.1.call-start = ((), (), s32[]{:S(2)}) async-start(), calls=%async_computation.6 | async-start | bytes 516096 | tf_op jit(solution)/shard_map/reduce_scatter | solution.py:60
  112.7 5.1 %copy-start.6 = (bf16[1344,2688]{1,0:T(8,128)(2,1)S(1)}, bf16[1344,2688]{1,0:T(8,128)(2,1)}, u32[]{:S(2)}) copy-start(bf16[1344,2688]{1,0:T(8,128)(2,1)} %all-gather.3.cloned.1.call-done) | copy-start | bytes 21676036
  119.4 3.1 copy-start.8
  131.2 109.6 %copy-start.5 = (u32[128]{0:T(128)S(1)}, u32[128]{0:T(128)}, u32[]{:S(2)}) copy-start(u32[128]{0:T(128)} %constant.95) | copy-start | bytes 1540
  232.3 12.9 %collective-permute-start = (bf16[1344,96]{0,1:T(8,128)(2,1)S(1)}, bf16[1344,96]{0,1:T(8,128)(2,1)S(1)}, u32[]{:S(2)}, u32[]{:S(2)}) collective-permute-start(bf16[1344,96]{0,1:T(8,128)(2,1)S(1)} %get-tuple-element.5), channel_id=1, source_target_pairs={{0,1},{1,2},{2,3},{3,4},{4,5},{5,6},{6,7},{7,8},{8,9},{9,10},{10,1... | collective-permute-start | bytes 774152
  235.2 10.0 %collective-permute-start.1 = (bf16[1344,84]{0,1:T(8,128)(2,1)S(1)}, bf16[1344,84]{0,1:T(8,128)(2,1)S(1)}, u32[]{:S(2)}, u32[]{:S(2)}) collective-permute-start(bf16[1344,84]{0,1:T(8,128)(2,1)S(1)} %slice.12), channel_id=1, source_target_pairs={{0,2},{1,3},{2,4},{3,5},{4,6},{5,7},{6,8},{7,9},{8,10},{9,11},{10,... | collective-permute-start | bytes 677384
  236.5 19.8 %collective-permute-start.2 = (bf16[96,1344]{1,0:T(8,128)(2,1)S(1)}, bf16[96,1344]{1,0:T(8,128)(2,1)S(1)}, u32[]{:S(2)}, u32[]{:S(2)}) collective-permute-start(bf16[96,1344]{1,0:T(8,128)(2,1)S(1)} %get-tuple-element.4), channel_id=1, source_target_pairs={{0,1},{1,2},{2,3},{3,4},{4,5},{5,6},{6,7},{7,8},{8,9},{9,10},{10,1... | collective-permute-start | bytes 774152
  242.1 14.2 %collective-permute-start.3 = (bf16[84,1344]{1,0:T(8,128)(2,1)S(1)}, bf16[84,1344]{1,0:T(8,128)(2,1)S(1)}, u32[]{:S(2)}, u32[]{:S(2)}) collective-permute-start(bf16[84,1344]{1,0:T(8,128)(2,1)S(1)} %slice.13), channel_id=1, source_target_pairs={{0,2},{1,3},{2,4},{3,5},{4,6},{5,7},{6,8},{7,9},{8,10},{9,11},{10,... | collective-permute-start | bytes 677384
  248.6 60.8 %copy-start.1 = (f32[1,168,84]{2,1,0:T(8,128)S(1)}, f32[1,168,84]{2,1,0:T(8,128)}, u32[]{:S(2)}) copy-start(f32[1,168,84]{2,1,0:T(8,128)} %param.10) | copy-start | bytes 169348
  248.9 71.8 %copy-start.4 = (f32[1,84,168]{2,0,1:T(1,128)S(1)}, f32[1,84,168]{2,0,1:T(1,128)}, u32[]{:S(2)}) copy-start(f32[1,84,168]{2,0,1:T(1,128)} %param.11) | copy-start | bytes 169348
  310.1 15.2 %all-to-all-start.3 = ((f32[8,1,84]{2,1,0:T(1,128)}), f32[8,1,84]{2,1,0:T(1,128)S(1)}, u32[]{:S(2)}, u32[]{:S(2)}) async-start(f32[8,1,84]{2,1,0:T(1,128)} %broadcast_in_dim.12), calls=%async_computation.4 | async-start | bytes 8192 | tf_op jit(solution)/shard_map/all_to_all | solution.py:21
Sparse Core Ops, SparseCore 0:
  55.2 57.3 all-gather.2
  261.7 29.0 reduce-scatter.5
where the time goes:
time: 334 us; the launch traced here: 333 us
  blocking collectives  153 us (46%)
  waiting for transfers between devices  77.1 us (23%)
  starting transfers between devices  46.5 us (14%)
  matrix products  18.5 us (6%)
  local copies, waits for them, and re-layouts  16.3 us (5%)
  between operations  15 us (4%)
  other arithmetic  6.88 us (2%)
    unnamed x1, blocking collectives  101 us
    psum x4, blocking collectives, one_axis_at_a_time(): value = lax.psum(value, axis)  34.1 us
    reduce_scatter x1, waiting for transfers between devices, sum_together(): lax.psum_scatter(lines, axis, tiled=True).reshape(-1)  29.3 us
    all_gather x1, waiting for transfers between devices, rows_first(): result = lax.all_gather(both, axis, axis=0, tiled=True)  19.6 us
    all_to_all x2, starting transfers between devices, sent_to_all(): return lax.all_to_all(copies, axis, split_axis=0, concat_axis=0, tiled=True)  17.4 us
    all_gather x1, blocking collectives, rows_first(): result = lax.all_gather(both, axis, axis=0, tiled=True)  17.3 us
    all_to_all x1, starting transfers between devices, local(): lax.all_to_all(clean.astype(jnp.bfloat16), 'row', split_axis=1, concat_ax...  13.5 us
    all_to_all x1, waiting for transfers between devices, local(): lax.all_to_all(noise.astype(jnp.bfloat16), 'row', split_axis=1, concat_ax...  11.6 us
  transfers between devices with their start and end apart: 10, of which 7 were waited for; matrix products, arithmetic and copies ran while one was open for 3% of the time, Pallas kernels for 0%

commit v1 on v0

--- a/solution.py
+++ b/solution.py
@@ -36,7 +36,9 @@
     turned = [jnp.moveaxis(a, dim, 0) for a, dim in zip(arrays, dims)]
     widths = [t[0].size for t in turned]
     both = jnp.concatenate([t.reshape(-1, w) for t, w in zip(turned, widths)], axis=1)
-    result = lax.all_gather(both, axis, axis=0, tiled=True)
+    result = jnp.concatenate(
+        lax.all_to_all(jnp.stack([both] * lax.axis_size(axis)), axis, 0, 0), axis=0
+    )
     blocks = jnp.split(result, [sum(widths[:k]) for k in range(1, len(widths))], axis=1)
     return tuple(
         (

time: 334 us -> 394 us (1.18)
  waiting for transfers between devices: 77.1 us -> 143 us
  blocking collectives: 153 us -> 134 us
  starting transfers between devices: 46.5 us -> 51.5 us
  local copies, waits for them, and re-layouts: 16.3 us -> 20.3 us
    all_to_all x0 -> x2, waiting for transfers between devices: none -> 90.8 us  [rows_first(): lax.all_to_all(jnp.stack([both] * lax.axis_size(axis)), axis, 0, 0)]
    all_gather x1 -> x0, waiting for transfers between devices: 19.6 us -> none  [rows_first(): result = lax.all_gather(both, axis, axis=0, tiled=True)]
    all_gather x1 -> x0, blocking collectives: 17.3 us -> none  [rows_first(): result = lax.all_gather(both, axis, axis=0, tiled=True)]
    all_to_all x0 -> x2, starting transfers between devices: none -> 9.56 us  [rows_first(): lax.all_to_all(jnp.stack([both] * lax.axis_size(axis)), axis, 0, 0)]
    all_to_all x1, waiting for transfers between devices: 11.6 us -> 5.94 us  [local(): lax.all_to_all(noise.astype(jnp.bfloat16), 'row', split_axis=1, concat_ax...]
    another operation x0 -> x2, local copies, waits for them, and re-layouts: none -> 4.57 us  [rows_first(): jnp.stack([both] * lax.axis_size(axis))]
    unnamed x28 -> x24, local copies, waits for them, and re-layouts: 8.61 us -> 8.13 us
  transfers between devices with their start and end apart: 10 -> 11, of which waited for: 7 -> 7; matrix products, arithmetic and copies ran while one was open for 3% -> 3% of each run, Pallas kernels for 0% -> 0%
where the time goes in v1:
time: 394 us; the launch traced here: 393 us
  waiting for transfers between devices  143 us (36%)
  blocking collectives  134 us (34%)
  starting transfers between devices  51.5 us (13%)
  matrix products  20.4 us (5%)
  local copies, waits for them, and re-layouts  20.3 us (5%)
  between operations  15.1 us (4%)
  other arithmetic  7.99 us (2%)
    unnamed x1, blocking collectives  100 us
    all_to_all x2, waiting for transfers between devices, rows_first(): lax.all_to_all(jnp.stack([both] * lax.axis_size(axis)), axis, 0, 0)  90.8 us
    psum x4, blocking collectives, one_axis_at_a_time(): value = lax.psum(value, axis)  34.2 us
    reduce_scatter x1, waiting for transfers between devices, sum_together(): lax.psum_scatter(lines, axis, tiled=True).reshape(-1)  29.2 us
    all_to_all x2, starting transfers between devices, sent_to_all(): return lax.all_to_all(copies, axis, split_axis=0, concat_axis=0, tiled=True)  17.4 us
    all_to_all x1, starting transfers between devices, local(): lax.all_to_all(clean.astype(jnp.bfloat16), 'row', split_axis=1, concat_ax...  9.78 us
    unnamed x4, starting transfers between devices  9.67 us
    all_to_all x2, starting transfers between devices, rows_first(): lax.all_to_all(jnp.stack([both] * lax.axis_size(axis)), axis, 0, 0)  9.56 us
  transfers between devices with their start and end apart: 11, of which 7 were waited for; matrix products, arithmetic and copies ran while one was open for 3% of the time, Pallas kernels for 0%

profile of v1, /device:TPU:1, one launch (start us, length us, event | category | flops | bytes accessed | tf_op | source)
XLA Modules:
  0.0 392.9 jit_solution(18048583715191568307)
XLA Ops:
  8.8 6.8 %all-to-all-start.2 = ((f32[8,1,84]{2,1,0:T(1,128)}), f32[8,1,84]{2,1,0:T(1,128)S(1)}, u32[]{:S(2)}, u32[]{:S(2)}) async-start(f32[8,1,84]{2,1,0:T(1,128)} %broadcast_in_dim.11), calls=%async_computation.2 | async-start | bytes 8192 | tf_op jit(solution)/shard_map/all_to_all | solution.py:21
  16.7 8.7 %psum.28 = f32[168]{0:T(256)S(1)} all-reduce(f32[168]{0:T(256)S(1)} %fusion.60), channel_id=1, replica_groups=mesh['row'=8,'col_0'=4,'col_1'=4] {'col_0'}, use_global_device_ids=true, to_apply=%region_3.0 | all-reduce | flops 168 | bytes 1344 | tf_op jit(solution)/shard_map/psum | solution.py:31
  25.5 8.5 %psum.29 = f32[168]{0:T(256)S(1)} all-reduce(f32[168]{0:T(256)S(1)} %psum.28), channel_id=1, replica_groups=mesh['row'=8,'col_0'=4,'col_1'=4] {'col_1'}, use_global_device_ids=true, to_apply=%region_4.0 | all-reduce | flops 168 | bytes 1344 | tf_op jit(solution)/shard_map/psum | solution.py:31
  36.2 3.7 all-to-all-start.3
  41.5 12.1 %all-to-all-done.3 = bf16[16,84,336]{2,1,0:T(8,128)(2,1)S(1)} async-done(((bf16[16,84,336]{2,1,0:T(8,128)(2,1)}), bf16[16,84,336]{2,1,0:T(8,128)(2,1)S(1)}, u32[]{:S(2)}, u32[]{:S(2)}) %all-to-all-start.3) | async-done | bytes 903200 | tf_op jit(solution)/shard_map/all_to_all | solution.py:40
  53.6 9.8 %all-to-all-start = ((bf16[168,8,128]{2,0,1:T(8,128)(2,1)}), bf16[168,8,128]{2,0,1:T(8,128)(2,1)}, u32[]{:S(2)}, u32[]{:S(2)}) async-start(bf16[168,8,128]{2,0,1:T(8,128)(2,1)} %copy_bitcast_fusion.2), calls=%async_computation | async-start | bytes 688128 | tf_op jit(solution)/shard_map/all_to_all | solution.py:102
  64.1 6.6 %all-to-all-done = bf16[168,8,128]{2,0,1:T(8,128)(2,1)} async-done(((bf16[168,8,128]{2,0,1:T(8,128)(2,1)}), bf16[168,8,128]{2,0,1:T(8,128)(2,1)}, u32[]{:S(2)}, u32[]{:S(2)}) %all-to-all-start) | async-done | bytes 344096 | tf_op jit(solution)/shard_map/all_to_all | solution.py:102
  70.7 5.1 %all-to-all-start.1 = ((bf16[168,8,128]{2,0,1:T(8,128)(2,1)}), bf16[168,8,128]{2,0,1:T(8,128)(2,1)}, u32[]{:S(2)}, u32[]{:S(2)}) async-start(bf16[168,8,128]{2,0,1:T(8,128)(2,1)} %copy_bitcast_fusion.1), calls=%async_computation.1 | async-start | bytes 688128 | tf_op jit(solution)/shard_map/all_to_all | solution.py:105
  77.3 5.9 %all-to-all-done.1 = bf16[168,8,128]{2,0,1:T(8,128)(2,1)} async-done(((bf16[168,8,128]{2,0,1:T(8,128)(2,1)}), bf16[168,8,128]{2,0,1:T(8,128)(2,1)}, u32[]{:S(2)}, u32[]{:S(2)}) %all-to-all-start.1) | async-done | bytes 344096 | tf_op jit(solution)/shard_map/all_to_all | solution.py:105
  83.2 3.5 stack.5
  86.7 5.9 %all-to-all-start.4 = ((bf16[8,168,2688]{2,1,0:T(8,128)(2,1)}), bf16[8,168,2688]{2,1,0:T(8,128)(2,1)}, u32[]{:S(2)}, u32[]{:S(2)}) async-start(bf16[8,168,2688]{2,1,0:T(8,128)(2,1)} %stack.5), calls=%async_computation.4 | async-start | bytes 14450688 | tf_op jit(solution)/shard_map/all_to_all | solution.py:40
  95.2 78.7 %all-to-all-done.4 = bf16[8,168,2688]{2,1,0:T(8,128)(2,1)} async-done(((bf16[8,168,2688]{2,1,0:T(8,128)(2,1)}), bf16[8,168,2688]{2,1,0:T(8,128)(2,1)}, u32[]{:S(2)}, u32[]{:S(2)}) %all-to-all-start.4) | async-done | bytes 7225376 | tf_op jit(solution)/shard_map/all_to_all | solution.py:40
  173.8 3.7 fusion.2
  178.8 3.7 fusion.38
  185.6 8.7 %convolution_convert_fusion.1 = bf16[1344,1344]{0,1:T(8,128)(2,1)} fusion(bf16[1344,128]{1,0:T(8,128)(2,1)S(1)} %get-tuple-element.12, f32[128,1344]{0,1:T(8,128)S(1)} %copy-done.7, bf16[128,1344]{0,1:T(8,128)(2,1)S(1)} %fusion.38, bf16[1344,2688]{1,0:T(8,128)(2,1)} %bitcast.12, f32[128,1344]{0,1:T(8,128)S(1)} %fusion.2), kind=kOutput, calls=%fused_computation.2 | convolution fusion | flops 928542720 | bytes 9461760 | tf_op jit(solution)/shard_map/dot_general | solution.py:135
  194.3 100.1 %fusion.75 = (bf16[96,1344]{1,0:T(8,128)(2,1)S(1)}, bf16[1344,96]{0,1:T(8,128)(2,1)S(1)}) fusion(bf16[1344,1344]{1,0:T(8,128)(2,1)} %convolution_convert_fusion, bf16[1344,1344]{0,1:T(8,128)(2,1)} %convolution_convert_fusion.1), kind=kCustom, calls=%all-reduce-scatter.2 | all-reduce-scatter fusion | flops 4128769 | bytes 7741952
  297.3 4.1 %collective-permute-start.2 = (bf16[96,1344]{1,0:T(8,128)(2,1)S(1)}, bf16[96,1344]{1,0:T(8,128)(2,1)S(1)}, u32[]{:S(2)}, u32[]{:S(2)}) collective-permute-start(bf16[96,1344]{1,0:T(8,128)(2,1)S(1)} %get-tuple-element.4), channel_id=1, source_target_pairs={{0,1},{1,2},{2,3},{3,4},{4,5},{5,6},{6,7},{7,8},{8,9},{9,10},{10,1... | collective-permute-start | bytes 774152
  305.5 3.1 concatenate.12
  309.3 7.2 %collective-permute-done.3 = bf16[84,1344]{1,0:T(8,128)(2,1)S(1)} collective-permute-done((bf16[84,1344]{1,0:T(8,128)(2,1)S(1)}, bf16[84,1344]{1,0:T(8,128)(2,1)S(1)}, u32[]{:S(2)}, u32[]{:S(2)}) %collective-permute-start.3) | collective-permute-done | bytes 225824
  321.7 29.2 %reduce-scatter.6.cloned.1.call-done = bf16[224,128]{1,0:T(8,128)(2,1)} async-done(((bf16[1792,128]{1,0:T(8,128)(2,1)}), bf16[224,128]{1,0:T(8,128)(2,1)}) %reduce-scatter.6.cloned.1.call-update) | async-done | bytes 57360 | tf_op jit(solution)/shard_map/reduce_scatter | solution.py:62
  352.4 8.6 %psum.30 = f32[168]{0:T(256)S(1)} all-reduce(f32[168]{0:T(256)S(1)} %fusion.62), channel_id=1, replica_groups=mesh['row'=8,'col_0'=4,'col_1'=4] {'col_0'}, use_global_device_ids=true, to_apply=%region_11.12 | all-reduce | flops 168 | bytes 1344 | tf_op jit(solution)/shard_map/psum | solution.py:31
  360.9 8.4 %psum.31 = f32[168]{0:T(256)S(1)} all-reduce(f32[168]{0:T(256)S(1)} %psum.30), channel_id=1, replica_groups=mesh['row'=8,'col_0'=4,'col_1'=4] {'col_1'}, use_global_device_ids=true, to_apply=%region_12.13 | all-reduce | flops 168 | bytes 1344 | tf_op jit(solution)/shard_map/psum | solution.py:31
  370.2 10.6 %all-to-all-start.5 = ((f32[8,1,84]{2,1,0:T(1,128)}), f32[8,1,84]{2,1,0:T(1,128)S(1)}, u32[]{:S(2)}, u32[]{:S(2)}) async-start(f32[8,1,84]{2,1,0:T(1,128)} %broadcast_in_dim.12), calls=%async_computation.6 | async-start | bytes 8192 | tf_op jit(solution)/shard_map/all_to_all | solution.py:21
  381.7 3.6 all-to-all-done.5
  (78 shorter events, 31.6 us)
Async XLA Ops:
  7.2 85.4 %copy-start = (s32[64]{0:T(128)S(1)}, s32[64]{0:T(128)}, u32[]{:S(2)}) copy-start(s32[64]{0:T(128)} %param.8) | copy-start | bytes 772
  7.2 32.8 %copy-start.2 = (f32[168,1024]{1,0:T(8,128)S(1)}, f32[168,1024]{1,0:T(8,128)}, u32[]{:S(2)}) copy-start(f32[168,1024]{1,0:T(8,128)} %param.6) | copy-start | bytes 2064388
  7.2 33.6 %copy-start.3 = (f32[168,1024]{1,0:T(8,128)S(1)}, f32[168,1024]{1,0:T(8,128)}, u32[]{:S(2)}) copy-start(f32[168,1024]{1,0:T(8,128)} %param.7) | copy-start | bytes 2064388
  8.8 25.2 %all-to-all-start.2 = ((f32[8,1,84]{2,1,0:T(1,128)}), f32[8,1,84]{2,1,0:T(1,128)S(1)}, u32[]{:S(2)}, u32[]{:S(2)}) async-start(f32[8,1,84]{2,1,0:T(1,128)} %broadcast_in_dim.11), calls=%async_computation.2 | async-start | bytes 8192 | tf_op jit(solution)/shard_map/all_to_all | solution.py:21
  36.2 17.4 %all-to-all-start.3 = ((bf16[16,84,336]{2,1,0:T(8,128)(2,1)}), bf16[16,84,336]{2,1,0:T(8,128)(2,1)S(1)}, u32[]{:S(2)}, u32[]{:S(2)}) async-start(bf16[16,84,336]{2,1,0:T(8,128)(2,1)} %stack.4), calls=%async_computation.3 | async-start | bytes 2162688 | tf_op jit(solution)/shard_map/all_to_all | solution.py:40
  53.6 17.1 %all-to-all-start = ((bf16[168,8,128]{2,0,1:T(8,128)(2,1)}), bf16[168,8,128]{2,0,1:T(8,128)(2,1)}, u32[]{:S(2)}, u32[]{:S(2)}) async-start(bf16[168,8,128]{2,0,1:T(8,128)(2,1)} %copy_bitcast_fusion.2), calls=%async_computation | async-start | bytes 688128 | tf_op jit(solution)/shard_map/all_to_all | solution.py:102
  70.7 12.5 %all-to-all-start.1 = ((bf16[168,8,128]{2,0,1:T(8,128)(2,1)}), bf16[168,8,128]{2,0,1:T(8,128)(2,1)}, u32[]{:S(2)}, u32[]{:S(2)}) async-start(bf16[168,8,128]{2,0,1:T(8,128)(2,1)} %copy_bitcast_fusion.1), calls=%async_computation.1 | async-start | bytes 688128 | tf_op jit(solution)/shard_map/all_to_all | solution.py:105
  86.7 87.2 %all-to-all-start.4 = ((bf16[8,168,2688]{2,1,0:T(8,128)(2,1)}), bf16[8,168,2688]{2,1,0:T(8,128)(2,1)}, u32[]{:S(2)}, u32[]{:S(2)}) async-start(bf16[8,168,2688]{2,1,0:T(8,128)(2,1)} %stack.5), calls=%async_computation.4 | async-start | bytes 14450688 | tf_op jit(solution)/shard_map/all_to_all | solution.py:40
  92.6 258.3 %reduce-scatter.6.cloned.1.call-start = ((), (), s32[]{:S(2)}) async-start(), calls=%async_computation.7 | async-start | bytes 516096 | tf_op jit(solution)/shard_map/reduce_scatter | solution.py:62
  92.6 85.0 %copy-start.6 = (f32[1,32,1344]{2,1,0:T(8,128)S(1)}, f32[1,32,1344]{2,1,0:T(8,128)}, u32[]{:S(2)}) copy-start(f32[1,32,1344]{2,1,0:T(8,128)} %param.9) | copy-start | bytes 516100
  182.5 3.1 copy-start.7
  194.3 107.1 %copy-start.5 = (u32[128]{0:T(128)S(1)}, u32[128]{0:T(128)}, u32[]{:S(2)}) copy-start(u32[128]{0:T(128)} %constant.95) | copy-start | bytes 1540
  294.4 11.1 %collective-permute-start = (bf16[1344,96]{0,1:T(8,128)(2,1)S(1)}, bf16[1344,96]{0,1:T(8,128)(2,1)S(1)}, u32[]{:S(2)}, u32[]{:S(2)}) collective-permute-start(bf16[1344,96]{0,1:T(8,128)(2,1)S(1)} %get-tuple-element.5), channel_id=1, source_target_pairs={{0,1},{1,2},{2,3},{3,4},{4,5},{5,6},{6,7},{7,8},{8,9},{9,10},{10,1... | collective-permute-start | bytes 774152
  295.8 9.7 %collective-permute-start.1 = (bf16[1344,84]{0,1:T(8,128)(2,1)S(1)}, bf16[1344,84]{0,1:T(8,128)(2,1)S(1)}, u32[]{:S(2)}, u32[]{:S(2)}) collective-permute-start(bf16[1344,84]{0,1:T(8,128)(2,1)S(1)} %slice.12), channel_id=1, source_target_pairs={{0,2},{1,3},{2,4},{3,5},{4,6},{5,7},{6,8},{7,9},{8,10},{9,11},{10,... | collective-permute-start | bytes 677384
  297.3 19.1 %collective-permute-start.2 = (bf16[96,1344]{1,0:T(8,128)(2,1)S(1)}, bf16[96,1344]{1,0:T(8,128)(2,1)S(1)}, u32[]{:S(2)}, u32[]{:S(2)}) collective-permute-start(bf16[96,1344]{1,0:T(8,128)(2,1)S(1)} %get-tuple-element.4), channel_id=1, source_target_pairs={{0,1},{1,2},{2,3},{3,4},{4,5},{5,6},{6,7},{7,8},{8,9},{9,10},{10,1... | collective-permute-start | bytes 774152
  302.7 13.7 %collective-permute-start.3 = (bf16[84,1344]{1,0:T(8,128)(2,1)S(1)}, bf16[84,1344]{1,0:T(8,128)(2,1)S(1)}, u32[]{:S(2)}, u32[]{:S(2)}) collective-permute-start(bf16[84,1344]{1,0:T(8,128)(2,1)S(1)} %slice.13), channel_id=1, source_target_pairs={{0,2},{1,3},{2,4},{3,5},{4,6},{5,7},{6,8},{7,9},{8,10},{9,11},{10,... | collective-permute-start | bytes 677384
  309.0 60.6 %copy-start.1 = (f32[1,168,84]{2,1,0:T(8,128)S(1)}, f32[1,168,84]{2,1,0:T(8,128)}, u32[]{:S(2)}) copy-start(f32[1,168,84]{2,1,0:T(8,128)} %param.10) | copy-start | bytes 169348
  309.2 71.5 %copy-start.4 = (f32[1,84,168]{2,0,1:T(1,128)S(1)}, f32[1,84,168]{2,0,1:T(1,128)}, u32[]{:S(2)}) copy-start(f32[1,84,168]{2,0,1:T(1,128)} %param.11) | copy-start | bytes 169348
  370.2 15.2 %all-to-all-start.5 = ((f32[8,1,84]{2,1,0:T(1,128)}), f32[8,1,84]{2,1,0:T(1,128)S(1)}, u32[]{:S(2)}, u32[]{:S(2)}) async-start(f32[8,1,84]{2,1,0:T(1,128)} %broadcast_in_dim.12), calls=%async_computation.6 | async-start | bytes 8192 | tf_op jit(solution)/shard_map/all_to_all | solution.py:21
Sparse Core Ops, SparseCore 0:
  321.8 29.0 reduce-scatter.5
